TPU v7x, 32 devices: a whole 2x2x4 slice. The times are simulated.
32 devices in a mesh: pr: 4 (over y, x), pc: 8 (over z, core).
Axes of the slice: x: 2, y: 2, z: 4, core: 2. Of those that a mesh axis runs over, the one named last changes fastest.
Arguments:
- pair_state: bfloat16 [96, 96, 128], P('pr', 'pc'), may hold values from -6 to 6
- left_weight: bfloat16 [128, 128], replicated, may hold values from -0.5 to 0.5
- right_weight: bfloat16 [128, 128], replicated, may hold values from -0.5 to 0.5
- mid_gain: float32 [128], replicated, may hold values from 0.25 to 1.75
- out_weight: bfloat16 [128, 128], replicated, may hold values from -0.5 to 0.5
- out_gate: bfloat16 [128, 128], replicated, may hold values from -0.5 to 0.5
Outputs:
- pair_update: bfloat16 [96, 96, 128], P('pr', 'pc')
All inputs are finite; a program needn't handle non-finite values.
Results may differ from a plain program's by a relative error of at most 0.012.
Values may be sent and summed in bfloat16 or wider, within the bound.
A program may use at most 128 MiB of HBM per device.

v0:
```python
import functools

import jax
import jax.numpy as jnp
from jax import lax
from jax.experimental import pallas as pl
from jax.experimental.pallas import tpu as pltpu
from jax.sharding import PartitionSpec as P

PIECES = 2
MESH = pl.DeviceIdType.MESH


def scale_channels(values, channel_gain):
    centred = values - jnp.mean(values, axis=-1, keepdims=True)
    return (
        centred
        * lax.rsqrt(jnp.mean(centred * centred, axis=-1, keepdims=True) + 1e-05)
        * channel_gain
    )


def project_pair(pair_in, left_weight, right_weight):
    left = jnp.einsum("ijc,cd->ijd", pair_in, left_weight, preferred_element_type=jnp.float32)
    right = jnp.einsum("ijc,cd->ijd", pair_in, right_weight, preferred_element_type=jnp.float32)
    return (pair_in, left.astype(jnp.bfloat16), right.astype(jnp.bfloat16))


def close_update(mixed, ready, mid_gain, out_weight, out_gate):
    scaled = scale_channels(mixed.astype(jnp.float32), mid_gain).astype(jnp.bfloat16)
    scaled = lax.optimization_barrier(scaled)
    gate = jax.nn.sigmoid(
        jnp.einsum("ijc,cd->ijd", ready, out_gate, preferred_element_type=jnp.float32)
    )
    return (
        jnp.einsum("ijd,dc->ijc", scaled, out_weight, preferred_element_type=jnp.float32) * gate
    ).astype(jnp.bfloat16)


def plain_body(pair_state, left_weight, right_weight, mid_gain, out_weight, out_gate):
    ready, left, right = project_pair(pair_state, left_weight, right_weight)
    count = pair_state.shape[0] * lax.axis_size("pr")
    left_lines, right_lines = (
        lax.all_to_all(left, "pr", split_axis=2, concat_axis=0, tiled=True),
        lax.all_to_all(right, "pr", split_axis=2, concat_axis=0, tiled=True),
    )
    strip = jnp.einsum(
        "kid,kjd->ijd",
        lax.all_gather(left_lines, "pc", axis=1, tiled=True),
        right_lines,
        preferred_element_type=jnp.float32,
    )
    strip = (strip * count ** (-0.5)).astype(jnp.bfloat16)
    mixed = lax.all_to_all(strip, "pr", split_axis=0, concat_axis=2, tiled=True)
    return close_update(mixed, ready, mid_gain, out_weight, out_gate)


def kernel(
    rows_of, line_of, J,
    x_hbm, wl_hbm, wr_hbm, gain_hbm, wo_hbm, wg_hbm, o_ref,
    xv, wl, wr, gain, wo, wg, xsib, zbuf, lbuf, rflat, rbuf, flat, mixed, gate, pout, pin,
    in_sem, x_send, x_recv, z_send, z_recv, r_send, p_send, p_recv, ready, ends,
):
    N, D = xv.shape[0] * xv.shape[1], xv.shape[2]
    K = N // J
    G = PIECES
    I = J // G
    part = I * J
    a = lax.axis_index("pr")
    c = lax.axis_index("pc")
    z, core = c // 2, c % 2
    sib = c + 1 - 2 * core
    way = 1 - 2 * (z // 2)
    inner = ((z + 1) % line_of) // 2
    middle = inner == 1
    near = z + way
    far = (z - way + line_of) % line_of
    third = (z + 2) % line_of
    across = a + 1 - 2 * (a % 2)
    along_y = (a + 2) % rows_of

    barrier = pltpu.get_barrier_semaphore()

    def greet(row, column):
        pl.semaphore_signal(barrier, inc=1, device_id=(row, column), device_id_type=MESH)

    greet(a, near * 2 + core)
    pl.when(middle)(lambda: greet(a, far * 2 + core))
    for row in (across, along_y):
        greet(row, c)
        greet(row, sib)
    greet(a, sib)
    loads = [
        pltpu.make_async_copy(s, d, in_sem.at[n])
        for n, (s, d) in enumerate(
            ((x_hbm, xv), (wr_hbm, wr), (wl_hbm, wl), (wg_hbm, wg), (gain_hbm, gain), (wo_hbm, wo))
        )
    ]
    for load in loads:
        load.start()
    for load in loads:
        load.wait()

    xs = xv[...].reshape(N, D)
    own = jnp.dot(xs, wr[...], preferred_element_type=jnp.float32)
    rflat[:N, :] = own
    lbuf[...] = jnp.dot(xs, wl[...], preferred_element_type=jnp.float32)
    gate[...] = jax.nn.sigmoid(jnp.dot(xs, wg[...], preferred_element_type=jnp.float32))

    pl.semaphore_wait(barrier, 6 + inner)

    def along(src, origin, g, target, sem):
        return pltpu.make_async_remote_copy(
            src_ref=src, dst_ref=zbuf.at[origin, g], send_sem=sem, recv_sem=z_recv.at[origin, g],
            device_id=(a, target * 2 + core), device_id_type=MESH,
        )

    def arrived(origin, g):
        pltpu.make_async_copy(xv.at[g], zbuf.at[origin, g], z_recv.at[origin, g]).wait()

    to_sib = pltpu.make_async_remote_copy(
        src_ref=xv, dst_ref=xsib, send_sem=x_send, recv_sem=x_recv,
        device_id=(a, sib), device_id_type=MESH,
    )
    to_sib.start()
    outward = [along(xv.at[g], z, g, far, z_send.at[1, g]) for g in range(G)]
    sent = [along(xv.at[g], z, g, near, z_send.at[0, g]) for g in range(G)]
    for copy in sent:
        copy.start()

    pl.semaphore_signal(ready, inc=1, device_id=(across, c), device_id_type=MESH)

    @pl.when(middle)
    def _():
        pl.semaphore_signal(ends, inc=1, device_id=(a, near * 2 + core), device_id_type=MESH)
        for copy in outward:
            copy.start()
        pl.semaphore_wait(ends, 1)
        pl.semaphore_signal(ends, inc=1, device_id=(a, far * 2 + core), device_id_type=MESH)

    @pl.when(jnp.logical_not(middle))
    def _():
        pl.semaphore_wait(ends, 1)
        for copy in outward:
            copy.start()

    to_sib.wait()
    rflat[N:, :] = jnp.dot(xsib[...].reshape(N, D), wr[...], preferred_element_type=jnp.float32)
    for k in range(K):
        rbuf[k] = rflat[pl.ds(k, 2 * J, stride=K), :]

    sums_sent = []

    def contract(t, origin, g, base):
        def step(k, sums):
            right = rbuf[k]
            return tuple(
                total + lbuf[pl.ds(base + i * K + k, 1), :] * right for i, total in enumerate(sums)
            )

        sums = lax.fori_loop(
            0, K, step, tuple(jnp.zeros((2 * J, D), jnp.float32) for _ in range(I)), unroll=K
        )
        for i in range(I):
            flat[i * J : (i + 1) * J, :] = sums[i][:J]
        pout[t, g, 0] = flat[:part, :].astype(pout.dtype)
        landing, sem = pin.at[g, core, a], p_recv.at[g, core, a]
        away = pltpu.make_async_remote_copy(
            src_ref=pout.at[t, g, 0], dst_ref=landing, send_sem=p_send.at[t, g, 0], recv_sem=sem,
            device_id=(origin, c), device_id_type=MESH,
        )
        here = pltpu.make_async_copy(pout.at[t, g, 0], landing, sem)
        side = pltpu.make_async_remote_copy(
            src_ref=pout.at[t, g, 1], dst_ref=landing, send_sem=p_send.at[t, g, 1], recv_sem=sem,
            device_id=(origin, sib), device_id_type=MESH,
        )
        pl.when(origin != a)(away.start)
        pl.when(origin == a)(here.start)
        for i in range(I):
            flat[part + i * J : part + (i + 1) * J, :] = sums[i][J:]
        pout[t, g, 1] = flat[part:, :].astype(pout.dtype)
        side.start()
        sums_sent.append((origin, away, side))

    def project(origin, g):
        block = zbuf[origin, g]
        lbuf[: I * K, :] = jnp.dot(block, wl[...], preferred_element_type=jnp.float32)

    pl.semaphore_wait(ready, 1)
    for g in range(G):
        contract(0, z, g, g * I * K)
    relays = []
    for g in range(G):
        arrived(near, g)
        first = along(zbuf.at[near, g], near, g, far, r_send.at[0, g])
        second = along(zbuf.at[far, g], far, g, near, r_send.at[1, g])
        relays += [first, second]

        @pl.when(middle)
        def _():
            first.start()
            arrived(far, g)
            second.start()

    for g in range(G):
        project(near, g)
        contract(1, near, g, 0)
    for g in range(G):

        @pl.when(jnp.logical_not(middle))
        def _():
            arrived(far, g)

        project(far, g)
        contract(2, far, g, 0)
        arrived(third, g)
        project(third, g)
        contract(3, third, g, 0)

    for g in range(G):
        totals = []
        for s in range(2):
            for row in range(rows_of):
                pltpu.make_async_copy(pout.at[0, 0, 0], pin.at[g, s, row], p_recv.at[g, s, row]).wait()
            total = pin[g, s, 0].astype(jnp.float32)
            for row in range(1, rows_of):
                total += pin[g, s, row].astype(jnp.float32)
            totals.append(total)
        total = jnp.concatenate(totals, axis=0) * (K * rows_of) ** (-0.5)
        total = total.astype(jnp.bfloat16).astype(jnp.float32)
        scaled = scale_channels(total, gain[...]).astype(jnp.bfloat16)
        out = jnp.dot(scaled, wo[...], preferred_element_type=jnp.float32)
        for s in range(2):
            for i in range(I):
                first_row = s * part + i * J
                mixed[pl.ds((s * G + g) * I + i, J, stride=K), :] = out[first_row : first_row + J]
    o_ref[...] = (mixed[...] * gate[...]).astype(o_ref.dtype)

    for copy in sent:
        copy.wait_send()

    for copy in outward:
        copy.wait_send()

    @pl.when(middle)
    def _():
        for copy in relays:
            copy.wait_send()

    for origin, away, side in sums_sent:
        pl.when(origin != a)(away.wait_send)
        side.wait_send()


def kernel_body(rows_of, line_of, pair_state, left_weight, right_weight, mid_gain, out_weight, out_gate):
    K, J, D = pair_state.shape
    N = K * J
    G = PIECES
    I = J // G
    f32, bf16 = jnp.float32, jnp.bfloat16
    anywhere = pl.BlockSpec(memory_space=pl.ANY)
    dma = pltpu.SemaphoreType.DMA
    pieces = jnp.transpose(pair_state, (1, 0, 2)).reshape(G, I * K, D)
    update = pl.pallas_call(
        functools.partial(kernel, rows_of, line_of, J),
        out_shape=jax.ShapeDtypeStruct((N, D), bf16),
        in_specs=[anywhere] * 6,
        out_specs=pl.BlockSpec(memory_space=pltpu.VMEM),
        scratch_shapes=[
            pltpu.VMEM((G, I * K, D), bf16),
            pltpu.VMEM((D, D), bf16),
            pltpu.VMEM((D, D), bf16),
            pltpu.VMEM((1, D), f32),
            pltpu.VMEM((D, D), bf16),
            pltpu.VMEM((D, D), bf16),
            pltpu.VMEM((G, I * K, D), bf16),
            pltpu.VMEM((line_of, G, I * K, D), bf16),
            pltpu.VMEM((N, D), f32),
            pltpu.VMEM((2 * N, D), f32),
            pltpu.VMEM((K, 2 * J, D), f32),
            pltpu.VMEM((2 * I * J, D), f32),
            pltpu.VMEM((N, D), f32),
            pltpu.VMEM((N, D), f32),
            pltpu.VMEM((line_of, G, 2, I * J, D), bf16),
            pltpu.VMEM((G, 2, rows_of, I * J, D), bf16),
            dma((6,)), dma, dma, dma((2, G)), dma((line_of, G)), dma((2, G)),
            dma((line_of, G, 2)), dma((G, 2, rows_of)), pltpu.SemaphoreType.REGULAR,
            pltpu.SemaphoreType.REGULAR,
        ],
        compiler_params=pltpu.CompilerParams(collective_id=0, has_side_effects=True),
    )(pieces, left_weight, right_weight, mid_gain.reshape(1, -1), out_weight, out_gate)
    return jnp.transpose(update.reshape(J, K, D), (1, 0, 2))


def body(rows_of, columns_of, *arrays):
    K, J, D = arrays[0].shape
    fits = (
        columns_of == 2 * rows_of
        and columns_of == 8
        and K == 2 * J
        and arrays[1].shape == (D, D)
        and D % 128 == 0
        and J <= 16
        and J % PIECES == 0
    )
    if fits:
        return kernel_body(rows_of, columns_of // 2, *arrays)
    return plain_body(*arrays)


def solution(mesh):
    placed = (P("pr", "pc", None), P(), P(), P(), P(), P())
    return jax.shard_map(
        functools.partial(body, mesh.shape["pr"], mesh.shape["pc"]),
        mesh=mesh, in_specs=placed, out_specs=P("pr", "pc", None), check_vma=False,
    )
```

profile of v0, /device:TPU:5, one launch (start us, length us, event | category | flops | bytes accessed | tf_op | source)
XLA Modules:
  0.0 17.1 jit_solution(1205900662322492370)
XLA Ops:
  0.0 15.5 %shard_map.64 = bf16[288,128]{1,0:T(8,128)(2,1)} custom-call(bf16[2,144,128]{2,1,0:T(8,128)(2,1)} %bitcast.8, bf16[128,128]{1,0:T(8,128)(2,1)} %wl_hbm.1, bf16[128,128]{1,0:T(8,128)(2,1)} %wr_hbm.1, f32[1,128]{1,0:T(1,128)} %bitcast.9, bf16[128,128]{1,0:T(8,128)(2,1)} %wo_hbm.1, bf16[128,128]{1,0:T(8,128)(2,1)} %wg_hbm.1), custom_call_target="tpu_custom_call" | custom-call | tf_op jit(solution)/shard_map/pallas_call | solution.py:264
  15.6 1.5 %copy.8 = bf16[24,12,128]{2,0,1:T(8,128)(2,1)} copy(bf16[24,12,128]{2,0,1:T(8,128)(2,1)} %bitcast.7) | data formatting | bytes 147456
where the time goes:
time: 17.3 us; the launch traced here: 17.1 us
  Pallas kernels  15.5 us (90%)
  local copies, waits for them, and re-layouts  1.52 us (9%)
    pallas_call x1, Pallas kernels, kernel_body(): pl.pallas_call(functools.partial(kernel, rows_of, line_of, J), out_shape=...  15.5 us
    unnamed x1, local copies, waits for them, and re-layouts  1.52 us

commit v1 on v0

--- a/solution.py
+++ b/solution.py
@@ -263,7 +263,7 @@
     pieces = jnp.transpose(pair_state, (1, 0, 2)).reshape(G, I * K, D)
     update = pl.pallas_call(
         functools.partial(kernel, rows_of, line_of, J),
-        out_shape=jax.ShapeDtypeStruct((N, D), bf16),
+        out_shape=pltpu.VMEM((N, D), bf16),
         in_specs=[anywhere] * 6,
         out_specs=pl.BlockSpec(memory_space=pltpu.VMEM),
         scratch_shapes=[

time: 17.3 us -> 15.7 us (0.908)
  local copies, waits for them, and re-layouts: 1.52 us -> 0.64 us
  Pallas kernels: 15.5 us -> 14.9 us
    unnamed x1, local copies, waits for them, and re-layouts: 1.52 us -> 0.64 us
    pallas_call x1, Pallas kernels: 15.5 us -> 14.9 us  [kernel_body(): pl.pallas_call(functools.partial(kernel, rows_of, line_of, J), out_shape=...]
where the time goes in v1:
time: 15.7 us; the launch traced here: 15.6 us
  Pallas kernels  14.9 us (95%)
  local copies, waits for them, and re-layouts  0.64 us (4%)
    pallas_call x1, Pallas kernels, kernel_body(): pl.pallas_call(functools.partial(kernel, rows_of, line_of, J), out_shape=...  14.9 us
    unnamed x1, local copies, waits for them, and re-layouts  0.64 us

profile of v1, /device:TPU:5, one launch (start us, length us, event | category | flops | bytes accessed | tf_op | source)
XLA Modules:
  0.0 15.6 jit_solution(1924322196044748596)
XLA Ops:
  0.0 14.9 %shard_map.64 = bf16[288,128]{1,0:T(8,128)(2,1)S(1)} custom-call(bf16[2,144,128]{2,1,0:T(8,128)(2,1)} %bitcast.8, bf16[128,128]{1,0:T(8,128)(2,1)} %wl_hbm.1, bf16[128,128]{1,0:T(8,128)(2,1)} %wr_hbm.1, f32[1,128]{1,0:T(1,128)} %bitcast.9, bf16[128,128]{1,0:T(8,128)(2,1)} %wo_hbm.1, bf16[128,128]{1,0:T(8,128)(2,1)} %wg_hbm.1), custom_call_target="tpu_custom_call" | custom-call | tf_op jit(solution)/shard_map/pallas_call | solution.py:264
  14.9 0.6 %copy.8 = bf16[24,12,128]{2,0,1:T(8,128)(2,1)} copy(bf16[24,12,128]{2,0,1:T(8,128)(2,1)S(1)} %bitcast.7) | data formatting | bytes 147456

commit v2 on v1

v2 whole, which is shorter than its diff:
```python
import functools

import jax
import jax.numpy as jnp
from jax import lax
from jax.experimental import pallas as pl
from jax.experimental.pallas import tpu as pltpu
from jax.sharding import PartitionSpec as P

PIECES = 3
MESH = pl.DeviceIdType.MESH


def whole(*chips):
    return tuple((chip, g) for chip in chips for g in range(PIECES))


def mixed(*chips):
    return tuple((chip, g) for g in range(PIECES) for chip in chips)


DOWN = (((), whole(0), whole(0, 1), mixed(0, 2, 1)), ((), whole(0), whole(1), mixed(0, 2, 1)))
UP = ((whole(1), whole(2), whole(3), ()), (whole(1), whole(2), whole(3), ()))
LATER = ((mixed(2, 3), whole(3), (), ()), (mixed(2, 3), (), (), ()))
ORDER = ((whole(1) + mixed(3, 2), mixed(0, 2, 3), mixed(1, 3, 0), whole(2) + mixed(1, 0)), (whole(1) + mixed(2, 3), mixed(0, 2, 3), mixed(3, 0, 1), whole(2) + mixed(0, 1)))


def scale_channels(values, channel_gain):
    centred = values - jnp.mean(values, axis=-1, keepdims=True)
    return (
        centred
        * lax.rsqrt(jnp.mean(centred * centred, axis=-1, keepdims=True) + 1e-05)
        * channel_gain
    )


def project_pair(pair_in, left_weight, right_weight):
    left = jnp.einsum("ijc,cd->ijd", pair_in, left_weight, preferred_element_type=jnp.float32)
    right = jnp.einsum("ijc,cd->ijd", pair_in, right_weight, preferred_element_type=jnp.float32)
    return (pair_in, left.astype(jnp.bfloat16), right.astype(jnp.bfloat16))


def close_update(mixed, ready, mid_gain, out_weight, out_gate):
    scaled = scale_channels(mixed.astype(jnp.float32), mid_gain).astype(jnp.bfloat16)
    scaled = lax.optimization_barrier(scaled)
    gate = jax.nn.sigmoid(
        jnp.einsum("ijc,cd->ijd", ready, out_gate, preferred_element_type=jnp.float32)
    )
    return (
        jnp.einsum("ijd,dc->ijc", scaled, out_weight, preferred_element_type=jnp.float32) * gate
    ).astype(jnp.bfloat16)


def plain_body(pair_state, left_weight, right_weight, mid_gain, out_weight, out_gate):
    ready, left, right = project_pair(pair_state, left_weight, right_weight)
    count = pair_state.shape[0] * lax.axis_size("pr")
    left_lines, right_lines = (
        lax.all_to_all(left, "pr", split_axis=2, concat_axis=0, tiled=True),
        lax.all_to_all(right, "pr", split_axis=2, concat_axis=0, tiled=True),
    )
    strip = jnp.einsum(
        "kid,kjd->ijd",
        lax.all_gather(left_lines, "pc", axis=1, tiled=True),
        right_lines,
        preferred_element_type=jnp.float32,
    )
    strip = (strip * count ** (-0.5)).astype(jnp.bfloat16)
    mixed = lax.all_to_all(strip, "pr", split_axis=0, concat_axis=2, tiled=True)
    return close_update(mixed, ready, mid_gain, out_weight, out_gate)


def kernel(
    rows_of, line_of, J,
    x_hbm, wl_hbm, wr_hbm, gain_hbm, wo_hbm, wg_hbm, o_ref,
    xv, wl, wr, gain, wo, wg, xsib, lv, zbuf, lbuf, rflat, rbuf, flat, merged, gate, pout, pin,
    in_sem, x_send, x_recv, z_send, z_recv, r_send, p_send, p_recv, ready, risen,
):
    N, D = xv.shape[0] * xv.shape[1], xv.shape[2]
    K = N // J
    G = PIECES
    I = J // G
    part = I * J
    last = line_of - 1
    a = lax.axis_index("pr")
    c = lax.axis_index("pc")
    z, core = c // 2, c % 2
    other = 1 - core
    sib = 2 * z + other
    p, q = a % 2, a // 2
    across, along_y, opposite = a + 1 - 2 * p, (a + 2) % rows_of, rows_of - 1 - a
    inner = ((z + 1) % line_of) // 2
    relaying = inner * core

    barrier = pltpu.get_barrier_semaphore()

    def tell(semaphore, row, column):
        pl.semaphore_signal(semaphore, inc=1, device_id=(row, column), device_id_type=MESH)

    def tell_chip(semaphore, row):
        tell(semaphore, row, c)
        tell(semaphore, row, sib)

    loads = [
        pltpu.make_async_copy(s, d, in_sem.at[n])
        for n, (s, d) in enumerate(
            ((x_hbm, xv), (wl_hbm, wl), (wr_hbm, wr), (wg_hbm, wg), (gain_hbm, gain), (wo_hbm, wo))
        )
    ]
    for load in loads:
        load.start()

    tell(barrier, a, sib)
    for level in range(1, line_of):

        @pl.when(z < level)
        def _():
            tell(barrier, a, 2 * level)
            tell(barrier, a, 2 * level + 1)

    pl.when(p == 0)(lambda: tell_chip(barrier, across))
    pl.when(q == 0)(lambda: tell_chip(barrier, along_y))
    pl.when(a == 0)(lambda: tell_chip(barrier, opposite))

    routes = [[sorted({chip for chip, g in DOWN[h][l] + UP[h][l] + LATER[h][l]}) for l in range(line_of)] for h in range(2)]

    def along(src, origin, half, g, column, sem):
        return pltpu.make_async_remote_copy(
            src_ref=src, dst_ref=zbuf.at[origin, half, g], send_sem=sem,
            recv_sem=z_recv.at[origin, half, g], device_id=(a, column), device_id_type=MESH,
        )

    def flow(half, level, target, g):
        between = 0 < level < last and 0 < target < last
        column = 2 * target + (1 if between else 1 - half)
        slot = routes[half][level].index(target)
        return along(lv.at[g], level, half, g, column, z_send.at[slot, g])

    def everywhere(act):
        for half in range(2):
            for level in range(line_of):
                if act.keywords["plan"][half][level]:
                    pl.when(jnp.logical_and(z == level, core == half))(functools.partial(act, half, level))

    def launch(half, level, plan):
        risen_to = level
        for target, g in plan[half][level]:
            if target > risen_to:
                for higher in range(risen_to + 1, target + 1):
                    if higher in [chip for chip, _ in plan[half][level]]:
                        pl.semaphore_wait(risen.at[higher], 2)
                risen_to = target
            flow(half, level, target, g).start()

    def arrived(origin, half, g):
        pltpu.make_async_copy(xv.at[0], zbuf.at[origin, half, g], z_recv.at[origin, half, g]).wait()

    to_sib = pltpu.make_async_remote_copy(
        src_ref=xv, dst_ref=xsib, send_sem=x_send, recv_sem=x_recv,
        device_id=(a, sib), device_id_type=MESH,
    )

    pl.semaphore_wait(barrier, 1 + 2 * z + 2 * (p + q + p * q))
    for level in range(1, line_of):

        @pl.when(z == level)
        def _():
            for half in range(2):
                for lower in (low for low in range(level) if level in routes[half][low]):
                    tell(risen.at[level], a, 2 * lower + half)

    pl.when(p == 1)(lambda: tell_chip(ready, across))
    pl.when(q == 1)(lambda: tell_chip(ready, along_y))
    pl.when(a == rows_of - 1)(lambda: tell_chip(ready, opposite))

    for load in loads[:2]:
        load.wait()
    to_sib.start()
    for g in range(G):
        rows = slice(g * I * K, (g + 1) * I * K)
        left = jnp.dot(xv[g], wl[...], preferred_element_type=jnp.float32)
        lbuf[rows, :] = left
        lv[g] = left.astype(lv.dtype)
    everywhere(functools.partial(launch, plan=DOWN))

    for load in loads[2:]:
        load.wait()
    xs = xv[...].reshape(N, D)
    rflat[:N, :] = jnp.dot(xs, wr[...], preferred_element_type=jnp.float32)
    gate[...] = jax.nn.sigmoid(jnp.dot(xs, wg[...], preferred_element_type=jnp.float32))

    everywhere(functools.partial(launch, plan=UP))
    to_sib.wait()
    rflat[N:, :] = jnp.dot(xsib[...].reshape(N, D), wr[...], preferred_element_type=jnp.float32)
    for k in range(K):
        rbuf[k] = rflat[pl.ds(k, 2 * J, stride=K), :]
    sums_sent = []

    def contract(t, origin, half, g, base):
        def step(k, sums):
            right = rbuf[k]
            return tuple(
                total + lbuf[pl.ds(base + i * K + k, 1), :] * right for i, total in enumerate(sums)
            )

        sums = lax.fori_loop(
            0, K, step, tuple(jnp.zeros((2 * J, D), jnp.float32) for _ in range(I)), unroll=K
        )
        landing, sem = pin.at[g, half, a], p_recv.at[g, half, a]
        away = pltpu.make_async_remote_copy(
            src_ref=pout.at[t, 0], dst_ref=landing, send_sem=p_send.at[t, 0], recv_sem=sem,
            device_id=(origin, c), device_id_type=MESH,
        )
        stay = pltpu.make_async_copy(pout.at[t, 0], landing, sem)
        side = pltpu.make_async_remote_copy(
            src_ref=pout.at[t, 1], dst_ref=landing, send_sem=p_send.at[t, 1], recv_sem=sem,
            device_id=(origin, sib), device_id_type=MESH,
        )
        for i in range(I):
            flat[i * J : (i + 1) * J, :] = sums[i][:J]
            flat[part + i * J : part + (i + 1) * J, :] = sums[i][J:]
        pout[t, 0] = flat[:part, :].astype(pout.dtype)
        pl.when(origin != a)(away.start)
        pl.when(origin == a)(stay.start)
        pout[t, 1] = flat[part:, :].astype(pout.dtype)
        side.start()
        sums_sent.append((origin, away, side))

    @pl.when(a < rows_of - 1)
    def _():
        pl.semaphore_wait(ready, 2 * ((1 - p) + (1 - q) + (1 - p) * (1 - q)))

    for g in range(G):
        contract(g, z, core, g, g * I * K)

    everywhere(functools.partial(launch, plan=LATER))

    peer = last - z
    outer = (peer + 2) % line_of
    relays = []
    for g in range(G):
        held = zbuf.at[peer, 1, g]
        relays.append(along(held, peer, 1, g, 2 * outer, r_send.at[0, g]))
        relays.append(along(held, peer, 1, g, sib, r_send.at[1, g]))

    @pl.when(relaying == 1)
    def _():
        for g in range(G):
            arrived(peer, 1, g)
            for copy in relays[2 * g : 2 * g + 2]:
                copy.start()

    def at_level(values):
        picked = values[0]
        for level in range(1, line_of):
            picked = picked + (z // level) * (1 - z // (level + 1)) * (values[level] - values[0])
        return picked

    def pick(lower, upper):
        return lower + core * (upper - lower)

    for n in range(last * G):
        origin, g = (
            pick(*(at_level([ORDER[half][level][n][e] for level in range(line_of)]) for half in range(2)))
            for e in range(2)
        )
        arrived(origin, other, g)
        lbuf[: I * K, :] = zbuf[origin, other, g].astype(jnp.float32)
        contract(G + n, origin, other, g, 0)

    for g in range(G):
        for s in range(2):
            for row in range(rows_of):
                pltpu.make_async_copy(pout.at[0, 0], pin.at[g, s, row], p_recv.at[g, s, row]).wait()
    for g in range(G):
        totals = []
        for s in range(2):
            total = pin[g, s, 0].astype(jnp.float32)
            for row in range(1, rows_of):
                total += pin[g, s, row].astype(jnp.float32)
            totals.append(total)
        total = jnp.concatenate(totals, axis=0) * (K * rows_of) ** (-0.5)
        total = total.astype(jnp.bfloat16).astype(jnp.float32)
        scaled = scale_channels(total, gain[...]).astype(jnp.bfloat16)
        out = jnp.dot(scaled, wo[...], preferred_element_type=jnp.float32)
        for s in range(2):
            for i in range(I):
                first_row = s * part + i * J
                merged[pl.ds((s * G + g) * I + i, J, stride=K), :] = out[first_row : first_row + J]
    o_ref[...] = (merged[...] * gate[...]).astype(o_ref.dtype)

    def settle(half, level, plan):
        for target in plan[half][level]:
            for g in range(G):
                flow(half, level, target, g).wait_send()

    everywhere(functools.partial(settle, plan=routes))

    @pl.when(relaying == 1)
    def _():
        for copy in relays:
            copy.wait_send()

    for origin, away, side in sums_sent:
        pl.when(origin != a)(away.wait_send)
        side.wait_send()


def kernel_body(rows_of, line_of, pair_state, left_weight, right_weight, mid_gain, out_weight, out_gate):
    K, J, D = pair_state.shape
    N = K * J
    G = PIECES
    I = J // G
    f32, bf16 = jnp.float32, jnp.bfloat16
    anywhere = pl.BlockSpec(memory_space=pl.ANY)
    dma = pltpu.SemaphoreType.DMA
    pieces = jnp.transpose(pair_state, (1, 0, 2)).reshape(G, I * K, D)
    update = pl.pallas_call(
        functools.partial(kernel, rows_of, line_of, J),
        out_shape=pltpu.VMEM((N, D), bf16),
        in_specs=[anywhere] * 6,
        out_specs=pl.BlockSpec(memory_space=pltpu.VMEM),
        scratch_shapes=[
            pltpu.VMEM((G, I * K, D), bf16),
            pltpu.VMEM((D, D), bf16),
            pltpu.VMEM((D, D), bf16),
            pltpu.VMEM((1, D), f32),
            pltpu.VMEM((D, D), bf16),
            pltpu.VMEM((D, D), bf16),
            pltpu.VMEM((G, I * K, D), bf16),
            pltpu.VMEM((G, I * K, D), bf16),
            pltpu.VMEM((line_of, 2, G, I * K, D), bf16),
            pltpu.VMEM((N, D), f32),
            pltpu.VMEM((2 * N, D), f32),
            pltpu.VMEM((K, 2 * J, D), f32),
            pltpu.VMEM((2 * I * J, D), f32),
            pltpu.VMEM((N, D), f32),
            pltpu.VMEM((N, D), f32),
            pltpu.VMEM((line_of * G, 2, I * J, D), bf16),
            pltpu.VMEM((G, 2, rows_of, I * J, D), bf16),
            dma((6,)), dma, dma, dma((3, G)), dma((line_of, 2, G)), dma((2, G)),
            dma((line_of * G, 2)), dma((G, 2, rows_of)), pltpu.SemaphoreType.REGULAR,
            pltpu.SemaphoreType.REGULAR((line_of,)),
        ],
        compiler_params=pltpu.CompilerParams(collective_id=0, has_side_effects=True),
    )(pieces, left_weight, right_weight, mid_gain.reshape(1, -1), out_weight, out_gate)
    return jnp.transpose(update.reshape(J, K, D), (1, 0, 2))


def body(rows_of, columns_of, *arrays):
    K, J, D = arrays[0].shape
    fits = (
        columns_of == 2 * rows_of
        and columns_of == 8
        and K == 2 * J
        and arrays[1].shape == (D, D)
        and D % 128 == 0
        and J <= 16
        and J % PIECES == 0
    )
    if fits:
        return kernel_body(rows_of, columns_of // 2, *arrays)
    return plain_body(*arrays)


def solution(mesh):
    placed = (P("pr", "pc", None), P(), P(), P(), P(), P())
    return jax.shard_map(
        functools.partial(body, mesh.shape["pr"], mesh.shape["pc"]),
        mesh=mesh, in_specs=placed, out_specs=P("pr", "pc", None), check_vma=False,
    )
```

time: 15.7 us -> 14.7 us (0.936)
  the two profiles are of different devices: /device:TPU:5 before, /device:TPU:24 now
where the time goes in v2:
time: 14.7 us; the launch traced here: 14.5 us
  Pallas kernels  13.9 us (95%)
  local copies, waits for them, and re-layouts  0.64 us (4%)
    pallas_call x1, Pallas kernels, kernel_body(): pl.pallas_call(functools.partial(kernel, rows_of, line_of, J), out_shape=...  13.9 us
    unnamed x1, local copies, waits for them, and re-layouts  0.64 us

profile of v2, /device:TPU:24, one launch (start us, length us, event | category | flops | bytes accessed | tf_op | source)
XLA Modules:
  0.0 14.5 jit_solution(6956077983439541185)
XLA Ops:
  0.0 13.9 %shard_map.64 = bf16[288,128]{1,0:T(8,128)(2,1)S(1)} custom-call(bf16[3,96,128]{2,1,0:T(8,128)(2,1)} %bitcast.8, bf16[128,128]{1,0:T(8,128)(2,1)} %wl_hbm.1, bf16[128,128]{1,0:T(8,128)(2,1)} %wr_hbm.1, f32[1,128]{1,0:T(1,128)} %bitcast.9, bf16[128,128]{1,0:T(8,128)(2,1)} %wo_hbm.1, bf16[128,128]{1,0:T(8,128)(2,1)} %wg_hbm.1), custom_call_target="tpu_custom_call" | custom-call | tf_op jit(solution)/shard_map/pallas_call | solution.py:317
  13.9 0.6 %copy.8 = bf16[24,12,128]{2,0,1:T(8,128)(2,1)} copy(bf16[24,12,128]{2,0,1:T(8,128)(2,1)S(1)} %bitcast.7) | data formatting | bytes 147456

commit v3 on v2

--- a/solution.py
+++ b/solution.py
@@ -22,7 +22,7 @@
 DOWN = (((), whole(0), whole(0, 1), mixed(0, 2, 1)), ((), whole(0), whole(1), mixed(0, 2, 1)))
 UP = ((whole(1), whole(2), whole(3), ()), (whole(1), whole(2), whole(3), ()))
 LATER = ((mixed(2, 3), whole(3), (), ()), (mixed(2, 3), (), (), ()))
-ORDER = ((whole(1) + mixed(3, 2), mixed(0, 2, 3), mixed(1, 3, 0), whole(2) + mixed(1, 0)), (whole(1) + mixed(2, 3), mixed(0, 2, 3), mixed(3, 0, 1), whole(2) + mixed(0, 1)))
+ORDER = ((whole(1) + mixed(3, 2), whole(0) + mixed(2, 3), whole(1) + mixed(3, 0), whole(2) + mixed(1, 0)), (whole(1) + mixed(2, 3), whole(0) + mixed(2, 3), mixed(3, 0) + whole(1), whole(2) + mixed(0, 1)))
 
 
 def scale_channels(values, channel_gain):
@@ -72,8 +72,8 @@
 def kernel(
     rows_of, line_of, J,
     x_hbm, wl_hbm, wr_hbm, gain_hbm, wo_hbm, wg_hbm, o_ref,
-    xv, wl, wr, gain, wo, wg, xsib, lv, zbuf, lbuf, rflat, rbuf, flat, merged, gate, pout, pin,
-    in_sem, x_send, x_recv, z_send, z_recv, r_send, p_send, p_recv, ready, risen,
+    xv, weights, gain, xsib, lv, zbuf, lbuf, rflat, rbuf, flat, merged, gate, pout, pin,
+    x_in, weights_in, gain_in, x_recv, z_sent, z_recv, p_sent, p_recv, ready, risen,
 ):
     N, D = xv.shape[0] * xv.shape[1], xv.shape[2]
     K = N // J
@@ -100,14 +100,12 @@
         tell(semaphore, row, c)
         tell(semaphore, row, sib)
 
-    loads = [
-        pltpu.make_async_copy(s, d, in_sem.at[n])
-        for n, (s, d) in enumerate(
-            ((x_hbm, xv), (wl_hbm, wl), (wr_hbm, wr), (wg_hbm, wg), (gain_hbm, gain), (wo_hbm, wo))
-        )
-    ]
-    for load in loads:
-        load.start()
+    load = pltpu.make_async_copy(x_hbm, xv, x_in)
+    load.start()
+    for n, weight in enumerate((wl_hbm, wr_hbm, wg_hbm, wo_hbm)):
+        pltpu.make_async_copy(weight, weights.at[n], weights_in).start()
+    load_gain = pltpu.make_async_copy(gain_hbm, gain, gain_in)
+    load_gain.start()
 
     tell(barrier, a, sib)
     for level in range(1, line_of):
@@ -121,19 +119,25 @@
     pl.when(q == 0)(lambda: tell_chip(barrier, along_y))
     pl.when(a == 0)(lambda: tell_chip(barrier, opposite))
 
-    routes = [[sorted({chip for chip, g in DOWN[h][l] + UP[h][l] + LATER[h][l]}) for l in range(line_of)] for h in range(2)]
-
-    def along(src, origin, half, g, column, sem):
+    routes = [
+        [sorted({chip for chip, g in DOWN[h][l] + UP[h][l] + LATER[h][l]}) for l in range(line_of)]
+        for h in range(2)
+    ]
+
+    def place(origin, half, g):
+        return zbuf.at[(origin * 2 + half) * G + g]
+
+    def along(src, origin, half, g, column, slot):
         return pltpu.make_async_remote_copy(
-            src_ref=src, dst_ref=zbuf.at[origin, half, g], send_sem=sem,
-            recv_sem=z_recv.at[origin, half, g], device_id=(a, column), device_id_type=MESH,
+            src_ref=src, dst_ref=place(origin, half, g), send_sem=z_sent,
+            recv_sem=z_recv.at[slot], device_id=(a, column), device_id_type=MESH,
         )
 
     def flow(half, level, target, g):
-        between = 0 < level < last and 0 < target < last
-        column = 2 * target + (1 if between else 1 - half)
-        slot = routes[half][level].index(target)
-        return along(lv.at[g], level, half, g, column, z_send.at[slot, g])
+        held = half == 1 and 0 < level < last and 0 < target < last
+        column = 2 * target + (1 if held else 1 - half)
+        slot = (last if held else (level - target - 1) % line_of) * G + g
+        return along(lv.at[g], level, half, g, column, slot)
 
     def everywhere(act):
         for half in range(2):
@@ -141,21 +145,24 @@
                 if act.keywords["plan"][half][level]:
                     pl.when(jnp.logical_and(z == level, core == half))(functools.partial(act, half, level))
 
-    def launch(half, level, plan):
-        risen_to = level
-        for target, g in plan[half][level]:
-            if target > risen_to:
-                for higher in range(risen_to + 1, target + 1):
-                    if higher in [chip for chip, _ in plan[half][level]]:
-                        pl.semaphore_wait(risen.at[higher], 2)
-                risen_to = target
+    def launch(half, level, plan, ready_to=None):
+        sends = plan[half][level]
+        if ready_to is not None:
+            ends = [next((n for n, s in enumerate(sends) if s[1] > g), len(sends)) for g in range(-1, G)]
+            sends = sends[ends[ready_to] : ends[ready_to + 1]]
+        seen = level
+        for target, g in sends:
+            if target > seen:
+                for higher in sorted({chip for chip, _ in sends if seen < chip <= target}):
+                    pl.semaphore_wait(risen.at[higher - 1], 2)
+                seen = target
             flow(half, level, target, g).start()
 
-    def arrived(origin, half, g):
-        pltpu.make_async_copy(xv.at[0], zbuf.at[origin, half, g], z_recv.at[origin, half, g]).wait()
+    def arrived(origin, half, g, slot):
+        pltpu.make_async_copy(xv.at[0], place(origin, half, g), z_recv.at[slot]).wait()
 
     to_sib = pltpu.make_async_remote_copy(
-        src_ref=xv, dst_ref=xsib, send_sem=x_send, recv_sem=x_recv,
+        src_ref=xv, dst_ref=xsib, send_sem=z_sent, recv_sem=x_recv,
         device_id=(a, sib), device_id_type=MESH,
     )
 
@@ -166,34 +173,33 @@
         def _():
             for half in range(2):
                 for lower in (low for low in range(level) if level in routes[half][low]):
-                    tell(risen.at[level], a, 2 * lower + half)
+                    tell(risen.at[level - 1], a, 2 * lower + half)
 
     pl.when(p == 1)(lambda: tell_chip(ready, across))
     pl.when(q == 1)(lambda: tell_chip(ready, along_y))
     pl.when(a == rows_of - 1)(lambda: tell_chip(ready, opposite))
 
-    for load in loads[:2]:
-        load.wait()
+    load.wait()
     to_sib.start()
+    pltpu.make_async_copy(weights, weights, weights_in).wait()
     for g in range(G):
         rows = slice(g * I * K, (g + 1) * I * K)
-        left = jnp.dot(xv[g], wl[...], preferred_element_type=jnp.float32)
+        left = jnp.dot(xv[g], weights[0], preferred_element_type=jnp.float32)
+        lv[g] = left.astype(lv.dtype)
+        everywhere(functools.partial(launch, plan=DOWN, ready_to=g))
         lbuf[rows, :] = left
-        lv[g] = left.astype(lv.dtype)
-    everywhere(functools.partial(launch, plan=DOWN))
-
-    for load in loads[2:]:
-        load.wait()
+
+    load_gain.wait()
     xs = xv[...].reshape(N, D)
-    rflat[:N, :] = jnp.dot(xs, wr[...], preferred_element_type=jnp.float32)
-    gate[...] = jax.nn.sigmoid(jnp.dot(xs, wg[...], preferred_element_type=jnp.float32))
+    rflat[:N, :] = jnp.dot(xs, weights[1], preferred_element_type=jnp.float32)
+    gate[...] = jax.nn.sigmoid(jnp.dot(xs, weights[2], preferred_element_type=jnp.float32))
 
     everywhere(functools.partial(launch, plan=UP))
-    to_sib.wait()
-    rflat[N:, :] = jnp.dot(xsib[...].reshape(N, D), wr[...], preferred_element_type=jnp.float32)
+    to_sib.wait_recv()
+    rflat[N:, :] = jnp.dot(xsib[...].reshape(N, D), weights[1], preferred_element_type=jnp.float32)
     for k in range(K):
         rbuf[k] = rflat[pl.ds(k, 2 * J, stride=K), :]
-    sums_sent = []
+
 
     def contract(t, origin, half, g, base):
         def step(k, sums):
@@ -205,25 +211,24 @@
         sums = lax.fori_loop(
             0, K, step, tuple(jnp.zeros((2 * J, D), jnp.float32) for _ in range(I)), unroll=K
         )
-        landing, sem = pin.at[g, half, a], p_recv.at[g, half, a]
+        landing, sem = pin.at[g, half, a], p_recv.at[g]
         away = pltpu.make_async_remote_copy(
-            src_ref=pout.at[t, 0], dst_ref=landing, send_sem=p_send.at[t, 0], recv_sem=sem,
+            src_ref=pout.at[2 * t], dst_ref=landing, send_sem=p_sent, recv_sem=sem,
             device_id=(origin, c), device_id_type=MESH,
         )
-        stay = pltpu.make_async_copy(pout.at[t, 0], landing, sem)
+        stay = pltpu.make_async_copy(pout.at[2 * t], landing, sem)
         side = pltpu.make_async_remote_copy(
-            src_ref=pout.at[t, 1], dst_ref=landing, send_sem=p_send.at[t, 1], recv_sem=sem,
+            src_ref=pout.at[2 * t + 1], dst_ref=landing, send_sem=p_sent, recv_sem=sem,
             device_id=(origin, sib), device_id_type=MESH,
         )
         for i in range(I):
             flat[i * J : (i + 1) * J, :] = sums[i][:J]
             flat[part + i * J : part + (i + 1) * J, :] = sums[i][J:]
-        pout[t, 0] = flat[:part, :].astype(pout.dtype)
+        pout[2 * t] = flat[:part, :].astype(pout.dtype)
         pl.when(origin != a)(away.start)
         pl.when(origin == a)(stay.start)
-        pout[t, 1] = flat[part:, :].astype(pout.dtype)
+        pout[2 * t + 1] = flat[part:, :].astype(pout.dtype)
         side.start()
-        sums_sent.append((origin, away, side))
 
     @pl.when(a < rows_of - 1)
     def _():
@@ -238,14 +243,14 @@
     outer = (peer + 2) % line_of
     relays = []
     for g in range(G):
-        held = zbuf.at[peer, 1, g]
-        relays.append(along(held, peer, 1, g, 2 * outer, r_send.at[0, g]))
-        relays.append(along(held, peer, 1, g, sib, r_send.at[1, g]))
+        held = place(peer, 1, g)
+        relays.append(along(held, peer, 1, g, 2 * outer, G + g))
+        relays.append(along(held, peer, 1, g, sib, (peer - z + last) % line_of * G + g))
 
     @pl.when(relaying == 1)
     def _():
         for g in range(G):
-            arrived(peer, 1, g)
+            arrived(peer, 1, g, last * G + g)
             for copy in relays[2 * g : 2 * g + 2]:
                 copy.start()
 
@@ -263,15 +268,12 @@
             pick(*(at_level([ORDER[half][level][n][e] for level in range(line_of)]) for half in range(2)))
             for e in range(2)
         )
-        arrived(origin, other, g)
-        lbuf[: I * K, :] = zbuf[origin, other, g].astype(jnp.float32)
+        arrived(origin, other, g, (origin - z + last) % line_of * G + g)
+        lbuf[: I * K, :] = zbuf[(origin * 2 + other) * G + g].astype(jnp.float32)
         contract(G + n, origin, other, g, 0)
 
     for g in range(G):
-        for s in range(2):
-            for row in range(rows_of):
-                pltpu.make_async_copy(pout.at[0, 0], pin.at[g, s, row], p_recv.at[g, s, row]).wait()
-    for g in range(G):
+        pltpu.make_async_copy(pin.at[g], pin.at[g], p_recv.at[g]).wait()
         totals = []
         for s in range(2):
             total = pin[g, s, 0].astype(jnp.float32)
@@ -281,7 +283,7 @@
         total = jnp.concatenate(totals, axis=0) * (K * rows_of) ** (-0.5)
         total = total.astype(jnp.bfloat16).astype(jnp.float32)
         scaled = scale_channels(total, gain[...]).astype(jnp.bfloat16)
-        out = jnp.dot(scaled, wo[...], preferred_element_type=jnp.float32)
+        out = jnp.dot(scaled, weights[3], preferred_element_type=jnp.float32)
         for s in range(2):
             for i in range(I):
                 first_row = s * part + i * J
@@ -289,20 +291,14 @@
     o_ref[...] = (merged[...] * gate[...]).astype(o_ref.dtype)
 
     def settle(half, level, plan):
-        for target in plan[half][level]:
-            for g in range(G):
-                flow(half, level, target, g).wait_send()
+        sends = (len(plan[half][level]) + 1) * G
+        held = [s for s in plan[half][level] if half == 1 and 0 < level < last and 0 < s < last]
+        sent = zbuf.at[pl.ds(0, sends + 2 * G * len(held))]
+        pltpu.make_async_copy(sent, sent, z_sent).wait()
 
     everywhere(functools.partial(settle, plan=routes))
-
-    @pl.when(relaying == 1)
-    def _():
-        for copy in relays:
-            copy.wait_send()
-
-    for origin, away, side in sums_sent:
-        pl.when(origin != a)(away.wait_send)
-        side.wait_send()
+    sent = pout.at[pl.ds(0, (2 * line_of - 1) * G)]
+    pltpu.make_async_copy(sent, sent, p_sent).wait()
 
 
 def kernel_body(rows_of, line_of, pair_state, left_weight, right_weight, mid_gain, out_weight, out_gate):
@@ -321,25 +317,21 @@
         out_specs=pl.BlockSpec(memory_space=pltpu.VMEM),
         scratch_shapes=[
             pltpu.VMEM((G, I * K, D), bf16),
-            pltpu.VMEM((D, D), bf16),
-            pltpu.VMEM((D, D), bf16),
+            pltpu.VMEM((4, D, D), bf16),
             pltpu.VMEM((1, D), f32),
-            pltpu.VMEM((D, D), bf16),
-            pltpu.VMEM((D, D), bf16),
             pltpu.VMEM((G, I * K, D), bf16),
             pltpu.VMEM((G, I * K, D), bf16),
-            pltpu.VMEM((line_of, 2, G, I * K, D), bf16),
+            pltpu.VMEM((line_of * 2 * G, I * K, D), bf16),
             pltpu.VMEM((N, D), f32),
             pltpu.VMEM((2 * N, D), f32),
             pltpu.VMEM((K, 2 * J, D), f32),
             pltpu.VMEM((2 * I * J, D), f32),
             pltpu.VMEM((N, D), f32),
             pltpu.VMEM((N, D), f32),
-            pltpu.VMEM((line_of * G, 2, I * J, D), bf16),
+            pltpu.VMEM((line_of * G * 2, I * J, D), bf16),
             pltpu.VMEM((G, 2, rows_of, I * J, D), bf16),
-            dma((6,)), dma, dma, dma((3, G)), dma((line_of, 2, G)), dma((2, G)),
-            dma((line_of * G, 2)), dma((G, 2, rows_of)), pltpu.SemaphoreType.REGULAR,
-            pltpu.SemaphoreType.REGULAR((line_of,)),
+            dma, dma, dma, dma, dma, dma((line_of * G,)), dma, dma((G,)),
+            pltpu.SemaphoreType.REGULAR, pltpu.SemaphoreType.REGULAR((line_of - 1,)),
         ],
         compiler_params=pltpu.CompilerParams(collective_id=0, has_side_effects=True),
     )(pieces, left_weight, right_weight, mid_gain.reshape(1, -1), out_weight, out_gate)

time: 14.7 us -> 13.9 us (0.946)
  Pallas kernels: 13.9 us -> 13.1 us
    pallas_call x1, Pallas kernels: 13.9 us -> 13.1 us  [kernel_body(): pl.pallas_call(functools.partial(kernel, rows_of, line_of, J), out_shape=...]
where the time goes in v3:
time: 13.9 us; the launch traced here: 13.7 us
  Pallas kernels  13.1 us (94%)
  local copies, waits for them, and re-layouts  0.64 us (5%)
    pallas_call x1, Pallas kernels, kernel_body(): pl.pallas_call(functools.partial(kernel, rows_of, line_of, J), out_shape=...  13.1 us
    unnamed x1, local copies, waits for them, and re-layouts  0.64 us

profile of v3, /device:TPU:24, one launch (start us, length us, event | category | flops | bytes accessed | tf_op | source)
XLA Modules:
  0.0 13.7 jit_solution(5793420147419036950)
XLA Ops:
  0.0 13.1 %shard_map.64 = bf16[288,128]{1,0:T(8,128)(2,1)S(1)} custom-call(bf16[3,96,128]{2,1,0:T(8,128)(2,1)} %bitcast.8, bf16[128,128]{1,0:T(8,128)(2,1)} %wl_hbm.1, bf16[128,128]{1,0:T(8,128)(2,1)} %wr_hbm.1, f32[1,128]{1,0:T(1,128)} %bitcast.9, bf16[128,128]{1,0:T(8,128)(2,1)} %wo_hbm.1, bf16[128,128]{1,0:T(8,128)(2,1)} %wg_hbm.1), custom_call_target="tpu_custom_call" | custom-call | tf_op jit(solution)/shard_map/pallas_call | solution.py:313
  13.1 0.6 %copy.8 = bf16[24,12,128]{2,0,1:T(8,128)(2,1)} copy(bf16[24,12,128]{2,0,1:T(8,128)(2,1)S(1)} %bitcast.7) | data formatting | bytes 147456

commit v4 on v3

--- a/solution.py
+++ b/solution.py
@@ -19,10 +19,23 @@
     return tuple((chip, g) for g in range(PIECES) for chip in chips)
 
 
-DOWN = (((), whole(0), whole(0, 1), mixed(0, 2, 1)), ((), whole(0), whole(1), mixed(0, 2, 1)))
-UP = ((whole(1), whole(2), whole(3), ()), (whole(1), whole(2), whole(3), ()))
-LATER = ((mixed(2, 3), whole(3), (), ()), (mixed(2, 3), (), (), ()))
-ORDER = ((whole(1) + mixed(3, 2), whole(0) + mixed(2, 3), whole(1) + mixed(3, 0), whole(2) + mixed(1, 0)), (whole(1) + mixed(2, 3), whole(0) + mixed(2, 3), mixed(3, 0) + whole(1), whole(2) + mixed(0, 1)))
+FIRST = (
+    (whole(1), whole(0, 2), whole(0, 1, 3), mixed(0, 2, 1)),
+    ((), whole(0, 2), whole(1), mixed(0, 2, 1)),
+)
+UP = (((), whole(3), (), ()), (whole(1), (), whole(3), ()))
+LATER = ((mixed(2, 3), (), (), ()), (mixed(2, 3), (), (), ()))
+GREET = (
+    (1, 1, 0, 0), (2, 1, 1, 0), (3, 1, 2, 0), (1, 1, 2, 1), (2, 1, 1, 1), (3, 1, 2, 1),
+)
+RISEN = (
+    (1, 1, 0, 0, 2), (2, 1, 0, 0, 3), (2, 1, 1, 0, 3),
+    (1, 0, 0, 1, 1), (2, 0, 0, 1, 2), (3, 0, 0, 1, 3), (3, 0, 2, 1, 3),
+)
+ORDER = (
+    (whole(1) + mixed(3, 2), whole(0) + mixed(2, 3), whole(1, 0, 3), whole(2) + mixed(1, 0)),
+    (whole(1) + mixed(2, 3), whole(0) + mixed(2, 3), whole(1, 0, 3), whole(2) + mixed(0, 1)),
+)
 
 
 def scale_channels(values, channel_gain):
@@ -91,6 +104,15 @@
     inner = ((z + 1) % line_of) // 2
     relaying = inner * core
 
+    def at_level(values):
+        picked = values[0]
+        for level in range(1, line_of):
+            picked = picked + (z // level) * (1 - z // (level + 1)) * (values[level] - values[0])
+        return picked
+
+    def pick(lower, upper):
+        return lower + core * (upper - lower)
+
     barrier = pltpu.get_barrier_semaphore()
 
     def tell(semaphore, row, column):
@@ -112,15 +134,20 @@
 
         @pl.when(z < level)
         def _():
-            tell(barrier, a, 2 * level)
-            tell(barrier, a, 2 * level + 1)
+            tell(barrier, a, 2 * level + other)
+
+    for level, half, target, end in GREET:
+
+        @pl.when(jnp.logical_and(z == level, core == half))
+        def _():
+            tell(barrier, a, 2 * target + end)
 
     pl.when(p == 0)(lambda: tell_chip(barrier, across))
     pl.when(q == 0)(lambda: tell_chip(barrier, along_y))
     pl.when(a == 0)(lambda: tell_chip(barrier, opposite))
 
     routes = [
-        [sorted({chip for chip, g in DOWN[h][l] + UP[h][l] + LATER[h][l]}) for l in range(line_of)]
+        [sorted({chip for chip, g in FIRST[h][l] + UP[h][l] + LATER[h][l]}) for l in range(line_of)]
         for h in range(2)
     ]
 
@@ -145,17 +172,12 @@
                 if act.keywords["plan"][half][level]:
                     pl.when(jnp.logical_and(z == level, core == half))(functools.partial(act, half, level))
 
-    def launch(half, level, plan, ready_to=None):
-        sends = plan[half][level]
-        if ready_to is not None:
-            ends = [next((n for n, s in enumerate(sends) if s[1] > g), len(sends)) for g in range(-1, G)]
-            sends = sends[ends[ready_to] : ends[ready_to + 1]]
-        seen = level
-        for target, g in sends:
-            if target > seen:
-                for higher in sorted({chip for chip, _ in sends if seen < chip <= target}):
-                    pl.semaphore_wait(risen.at[higher - 1], 2)
-                seen = target
+    def launch(half, level, plan):
+        seen = set()
+        for target, g in plan[half][level]:
+            if target not in seen and any(entry[2:] == (level, half, target) for entry in RISEN):
+                pl.semaphore_wait(risen.at[target - 1], 1)
+            seen.add(target)
             flow(half, level, target, g).start()
 
     def arrived(origin, half, g, slot):
@@ -166,14 +188,16 @@
         device_id=(a, sib), device_id_type=MESH,
     )
 
-    pl.semaphore_wait(barrier, 1 + 2 * z + 2 * (p + q + p * q))
-    for level in range(1, line_of):
-
-        @pl.when(z == level)
+    greeted = [
+        [1 + l + sum(entry[2:] == (l, h) for entry in GREET) for h in range(2)] for l in range(line_of)
+    ]
+    lower, upper = (at_level([greeted[l][h] for l in range(line_of)]) for h in range(2))
+    pl.semaphore_wait(barrier, pick(lower, upper) + 2 * (p + q + p * q))
+    for level, half, target, end, chip in RISEN:
+
+        @pl.when(jnp.logical_and(z == level, core == half))
         def _():
-            for half in range(2):
-                for lower in (low for low in range(level) if level in routes[half][low]):
-                    tell(risen.at[level - 1], a, 2 * lower + half)
+            tell(risen.at[chip - 1], a, 2 * target + end)
 
     pl.when(p == 1)(lambda: tell_chip(ready, across))
     pl.when(q == 1)(lambda: tell_chip(ready, along_y))
@@ -186,9 +210,8 @@
         rows = slice(g * I * K, (g + 1) * I * K)
         left = jnp.dot(xv[g], weights[0], preferred_element_type=jnp.float32)
         lv[g] = left.astype(lv.dtype)
-        everywhere(functools.partial(launch, plan=DOWN, ready_to=g))
         lbuf[rows, :] = left
-
+    everywhere(functools.partial(launch, plan=FIRST))
     load_gain.wait()
     xs = xv[...].reshape(N, D)
     rflat[:N, :] = jnp.dot(xs, weights[1], preferred_element_type=jnp.float32)
@@ -254,15 +277,6 @@
             for copy in relays[2 * g : 2 * g + 2]:
                 copy.start()
 
-    def at_level(values):
-        picked = values[0]
-        for level in range(1, line_of):
-            picked = picked + (z // level) * (1 - z // (level + 1)) * (values[level] - values[0])
-        return picked
-
-    def pick(lower, upper):
-        return lower + core * (upper - lower)
-
     for n in range(last * G):
         origin, g = (
             pick(*(at_level([ORDER[half][level][n][e] for level in range(line_of)]) for half in range(2)))
@@ -273,7 +287,8 @@
         contract(G + n, origin, other, g, 0)
 
     for g in range(G):
-        pltpu.make_async_copy(pin.at[g], pin.at[g], p_recv.at[g]).wait()
+        for ahead in ([0] if g == 0 else range(1, G) if g == 1 else []):
+            pltpu.make_async_copy(pin.at[ahead], pin.at[ahead], p_recv.at[ahead]).wait()
         totals = []
         for s in range(2):
             total = pin[g, s, 0].astype(jnp.float32)

time: 13.9 us -> 13.8 us (level)
  the two profiles are of different devices: /device:TPU:24 before, /device:TPU:5 now
where the time goes in v4:
time: 13.8 us; the launch traced here: 13.7 us
  Pallas kernels  13 us (94%)
  local copies, waits for them, and re-layouts  0.64 us (5%)
    pallas_call x1, Pallas kernels, kernel_body(): pl.pallas_call(functools.partial(kernel, rows_of, line_of, J), out_shape=...  13 us
    unnamed x1, local copies, waits for them, and re-layouts  0.64 us

profile of v4, /device:TPU:5, one launch (start us, length us, event | category | flops | bytes accessed | tf_op | source)
XLA Modules:
  0.0 13.7 jit_solution(12460351691887442364)
XLA Ops:
  0.0 13.0 %shard_map.64 = bf16[288,128]{1,0:T(8,128)(2,1)S(1)} custom-call(bf16[3,96,128]{2,1,0:T(8,128)(2,1)} %bitcast.8, bf16[128,128]{1,0:T(8,128)(2,1)} %wl_hbm.1, bf16[128,128]{1,0:T(8,128)(2,1)} %wr_hbm.1, f32[1,128]{1,0:T(1,128)} %bitcast.9, bf16[128,128]{1,0:T(8,128)(2,1)} %wo_hbm.1, bf16[128,128]{1,0:T(8,128)(2,1)} %wg_hbm.1), custom_call_target="tpu_custom_call" | custom-call | tf_op jit(solution)/shard_map/pallas_call | solution.py:328
  13.0 0.6 %copy.8 = bf16[24,12,128]{2,0,1:T(8,128)(2,1)} copy(bf16[24,12,128]{2,0,1:T(8,128)(2,1)S(1)} %bitcast.7) | data formatting | bytes 147456

commit v5 on v4

--- a/solution.py
+++ b/solution.py
@@ -34,7 +34,7 @@
 )
 ORDER = (
     (whole(1) + mixed(3, 2), whole(0) + mixed(2, 3), whole(1, 0, 3), whole(2) + mixed(1, 0)),
-    (whole(1) + mixed(2, 3), whole(0) + mixed(2, 3), whole(1, 0, 3), whole(2) + mixed(0, 1)),
+    (whole(1) + mixed(2, 3), whole(0) + mixed(3, 2), whole(1, 0, 3), whole(2) + mixed(0, 1)),
 )
 
 
@@ -86,7 +86,7 @@
     rows_of, line_of, J,
     x_hbm, wl_hbm, wr_hbm, gain_hbm, wo_hbm, wg_hbm, o_ref,
     xv, weights, gain, xsib, lv, zbuf, lbuf, rflat, rbuf, flat, merged, gate, pout, pin,
-    x_in, weights_in, gain_in, x_recv, z_sent, z_recv, p_sent, p_recv, ready, risen,
+    x_recv, z_sent, z_recv, p_sent, p_recv, ready, risen,
 ):
     N, D = xv.shape[0] * xv.shape[1], xv.shape[2]
     K = N // J
@@ -122,12 +122,11 @@
         tell(semaphore, row, c)
         tell(semaphore, row, sib)
 
-    load = pltpu.make_async_copy(x_hbm, xv, x_in)
+    load = pltpu.make_async_copy(x_hbm, xv, z_sent)
     load.start()
     for n, weight in enumerate((wl_hbm, wr_hbm, wg_hbm, wo_hbm)):
-        pltpu.make_async_copy(weight, weights.at[n], weights_in).start()
-    load_gain = pltpu.make_async_copy(gain_hbm, gain, gain_in)
-    load_gain.start()
+        pltpu.make_async_copy(weight, weights.at[n], p_sent).start()
+    load_gain = pltpu.make_async_copy(gain_hbm, gain, p_sent)
 
     tell(barrier, a, sib)
     for level in range(1, line_of):
@@ -205,20 +204,19 @@
 
     load.wait()
     to_sib.start()
-    pltpu.make_async_copy(weights, weights, weights_in).wait()
-    for g in range(G):
-        rows = slice(g * I * K, (g + 1) * I * K)
-        left = jnp.dot(xv[g], weights[0], preferred_element_type=jnp.float32)
-        lv[g] = left.astype(lv.dtype)
-        lbuf[rows, :] = left
+    pltpu.make_async_copy(weights, weights, p_sent).wait()
+    load_gain.start()
+    xs = xv[...].reshape(N, D)
+    left = jnp.dot(xs, weights[0], preferred_element_type=jnp.float32)
+    lv[...] = left.astype(lv.dtype).reshape(lv.shape)
     everywhere(functools.partial(launch, plan=FIRST))
-    load_gain.wait()
-    xs = xv[...].reshape(N, D)
+    lbuf[...] = left
     rflat[:N, :] = jnp.dot(xs, weights[1], preferred_element_type=jnp.float32)
     gate[...] = jax.nn.sigmoid(jnp.dot(xs, weights[2], preferred_element_type=jnp.float32))
 
     everywhere(functools.partial(launch, plan=UP))
     to_sib.wait_recv()
+    load_gain.wait()
     rflat[N:, :] = jnp.dot(xsib[...].reshape(N, D), weights[1], preferred_element_type=jnp.float32)
     for k in range(K):
         rbuf[k] = rflat[pl.ds(k, 2 * J, stride=K), :]
@@ -345,7 +343,7 @@
             pltpu.VMEM((N, D), f32),
             pltpu.VMEM((line_of * G * 2, I * J, D), bf16),
             pltpu.VMEM((G, 2, rows_of, I * J, D), bf16),
-            dma, dma, dma, dma, dma, dma((line_of * G,)), dma, dma((G,)),
+            dma, dma, dma((line_of * G,)), dma, dma((G,)),
             pltpu.SemaphoreType.REGULAR, pltpu.SemaphoreType.REGULAR((line_of - 1,)),
         ],
         compiler_params=pltpu.CompilerParams(collective_id=0, has_side_effects=True),

time: 13.8 us -> 13.8 us (level)
  no operation moved by 1% of the time
where the time goes in v5:
time: 13.8 us; the launch traced here: 13.6 us
  Pallas kernels  13 us (94%)
  local copies, waits for them, and re-layouts  0.64 us (5%)
    pallas_call x1, Pallas kernels, kernel_body(): pl.pallas_call(functools.partial(kernel, rows_of, line_of, J), out_shape=...  13 us
    unnamed x1, local copies, waits for them, and re-layouts  0.64 us

profile of v5, /device:TPU:5, one launch (start us, length us, event | category | flops | bytes accessed | tf_op | source)
XLA Modules:
  0.0 13.6 jit_solution(13238158788324985426)
XLA Ops:
  0.0 13.0 %shard_map.64 = bf16[288,128]{1,0:T(8,128)(2,1)S(1)} custom-call(bf16[3,96,128]{2,1,0:T(8,128)(2,1)} %bitcast.8, bf16[128,128]{1,0:T(8,128)(2,1)} %wl_hbm.1, bf16[128,128]{1,0:T(8,128)(2,1)} %wr_hbm.1, f32[1,128]{1,0:T(1,128)} %bitcast.9, bf16[128,128]{1,0:T(8,128)(2,1)} %wo_hbm.1, bf16[128,128]{1,0:T(8,128)(2,1)} %wg_hbm.1), custom_call_target="tpu_custom_call" | custom-call | tf_op jit(solution)/shard_map/pallas_call | solution.py:326
  13.0 0.6 %copy.8 = bf16[24,12,128]{2,0,1:T(8,128)(2,1)} copy(bf16[24,12,128]{2,0,1:T(8,128)(2,1)S(1)} %bitcast.7) | data formatting | bytes 147456
